TPU v7x, 32 devices: a whole 2x2x4 slice. The times are simulated.
32 devices in a mesh: bank: 4 (over z), zero: 8 (over y, x, core).
Axes of the slice: x: 2, y: 2, z: 4, core: 2. Of those that a mesh axis runs over, the one named last changes fastest.
Arguments:
- train_gate: float32 [64, 2048, 1408], P('bank', 'zero'), may hold values from -0.1875 to 0.1875
- train_up: float32 [64, 2048, 1408], P('bank', 'zero'), may hold values from -0.1875 to 0.1875
- router_weight: float32 [2048, 64], P('zero', 'bank'), may hold values from -0.125 to 0.125
- router_gain: float32 [2048], P('zero'), may hold values from 0.25 to 1.75
Outputs:
- ready_gate: bfloat16 [64, 2048, 1408], P('bank', None, 'zero')
- ready_up: bfloat16 [64, 2048, 1408], P('bank', None, 'zero')
- scale_gate: float32 [64, 1408], P('bank', 'zero')
- scale_up: float32 [64, 1408], P('bank', 'zero')
- serve_router: bfloat16 [2048, 64], replicated
All inputs are finite; a program needn't handle non-finite values. Where the computation divides by a largest or mean magnitude, that divisor is 1e-20 or more.
Results may differ from a plain program's by a relative error of at most 0.012.
Values may be sent and summed in bfloat16 or wider, within the bound.
A program may use at most 192 MiB of HBM per device.

v0:
```python
import jax
import jax.numpy as jnp
from jax import lax
from jax.sharding import PartitionSpec as P

D_MODEL = 2048


def local(train_gate, train_up, router_weight, router_gain):
    total_gate, total_up = (
        lax.psum(jnp.sum(jnp.abs(train_gate), axis=1).astype(jnp.bfloat16), "zero").astype(
            jnp.float32
        ),
        lax.psum(jnp.sum(jnp.abs(train_up), axis=1).astype(jnp.bfloat16), "zero").astype(
            jnp.float32
        ),
    )
    scale_gate = total_gate / D_MODEL
    scale_up = total_up / D_MODEL
    narrow_gate, narrow_up = (
        (train_gate / jnp.expand_dims(scale_gate, 1)).astype(jnp.bfloat16),
        (train_up / jnp.expand_dims(scale_up, 1)).astype(jnp.bfloat16),
    )
    ready_gate, ready_up = (
        lax.all_to_all(narrow_gate, "zero", split_axis=2, concat_axis=1, tiled=True),
        lax.all_to_all(narrow_up, "zero", split_axis=2, concat_axis=1, tiled=True),
    )
    scale_gate = lax.dynamic_slice_in_dim(
        scale_gate, lax.axis_index("zero") * ready_gate.shape[2], ready_gate.shape[2], axis=1
    )
    scale_up = lax.dynamic_slice_in_dim(
        scale_up, lax.axis_index("zero") * ready_up.shape[2], ready_up.shape[2], axis=1
    )
    part_router = (router_weight * router_gain[:, None]).astype(jnp.bfloat16)
    row_router = lax.all_gather(part_router, "zero", axis=0, tiled=True)
    serve_router = lax.all_gather(row_router, "bank", axis=1, tiled=True)
    return (ready_gate, ready_up, scale_gate, scale_up, serve_router)


def solution(mesh):
    in_specs = (P("bank", "zero", None), P("bank", "zero", None), P("zero", "bank"), P("zero"))
    out_specs = (
        P("bank", None, "zero"),
        P("bank", None, "zero"),
        P("bank", "zero"),
        P("bank", "zero"),
        P(),
    )
    return jax.shard_map(local, mesh=mesh, in_specs=in_specs, out_specs=out_specs, check_vma=False)
```

profile of v0, /device:TPU:0, one launch (start us, length us, event | category | flops | bytes accessed | tf_op | source)
XLA Modules:
  0.0 443.6 jit_solution(4854745292164101)
XLA Ops:
  7.2 0.0 all-reduce.3.cloned.1.call-start
  7.2 16.0 %abs_reduce_fusion = (bf16[16,1408]{1,0:T(8,128)(2,1)}, bf16[16,1408]{1,0:T(8,128)(2,1)}) fusion(f32[16,256,1408]{2,1,0:T(8,128)} %param.5, f32[16,256,1408]{2,1,0:T(8,128)} %param.4), kind=kLoop, calls=%fused_computation.1 | loop fusion | flops 23023616 | bytes 46227456 | tf_op jit(solution)/shard_map/reduce_sum | solution.py:14
  23.2 0.0 all-reduce.3.cloned.1.call-update
  23.2 23.7 %copy.22 = f32[16,256,1408]{1,0,2:T(8,128)} copy(f32[16,256,1408]{2,1,0:T(8,128)} %param.5) | data formatting | bytes 46137344 | tf_op args[1]
  46.9 30.6 %all-reduce.3.cloned.1.call-done = (bf16[16,1408]{1,0:T(8,128)(2,1)}, bf16[16,1408]{1,0:T(8,128)(2,1)}) async-done(((bf16[16,1408]{1,0:T(8,128)(2,1)}, bf16[16,1408]{1,0:T(8,128)(2,1)}), (bf16[16,1408]{1,0:T(8,128)(2,1)}, bf16[16,1408]{1,0:T(8,128)(2,1)})) %all-reduce.3.cloned.1.call-update) | async-done | bytes 90128 | tf_op jit(solution)/shard_map/psum | solution.py:11
  77.6 0.8 convert_multiply_fusion
  78.4 0.3 copy.21
  78.7 14.2 %divide_convert_fusion = bf16[16,256,1408]{1,0,2:T(8,128)(2,1)} fusion(f32[16,256,1408]{1,0,2:T(8,128)} %copy.22, f32[16,1408]{0,1:T(8,128)S(1)} %copy.21), kind=kLoop, calls=%fused_computation | loop fusion | flops 11534336 | bytes 34693120 | tf_op jit(solution)/shard_map/convert_element_type | solution.py:22
  92.9 5.2 %all-to-all-start.1 = ((bf16[16,256,1408]{1,0,2:T(8,128)(2,1)}), bf16[16,256,1408]{1,0,2:T(8,128)(2,1)}, u32[]{:S(2)}, u32[]{:S(2)}) async-start(bf16[16,256,1408]{1,0,2:T(8,128)(2,1)} %divide_convert_fusion), calls=%async_computation.1 | async-start | bytes 23068672 | tf_op jit(solution)/shard_map/all_to_all | solution.py:26
  98.1 23.7 %copy.18 = f32[16,256,1408]{1,0,2:T(8,128)} copy(f32[16,256,1408]{2,1,0:T(8,128)} %param.4) | data formatting | bytes 46137344 | tf_op args[0]
  121.8 0.3 copy.17
  122.1 0.0 copy-start.1
  122.1 14.2 %divide_convert_fusion.1 = bf16[16,256,1408]{1,0,2:T(8,128)(2,1)} fusion(f32[16,256,1408]{1,0,2:T(8,128)} %copy.18, f32[16,1408]{0,1:T(8,128)S(1)} %copy.17), kind=kLoop, calls=%fused_computation.2 | loop fusion | flops 11534336 | bytes 34693120 | tf_op jit(solution)/shard_map/convert_element_type | solution.py:21
  136.3 89.5 %all-to-all-done.1 = bf16[16,256,1408]{1,0,2:T(8,128)(2,1)} async-done(((bf16[16,256,1408]{1,0,2:T(8,128)(2,1)}), bf16[16,256,1408]{1,0,2:T(8,128)(2,1)}, u32[]{:S(2)}, u32[]{:S(2)}) %all-to-all-start.1) | async-done | bytes 11534368 | tf_op jit(solution)/shard_map/all_to_all | solution.py:26
  225.9 5.3 %all-to-all-start = ((bf16[16,256,1408]{1,0,2:T(8,128)(2,1)}), bf16[16,256,1408]{1,0,2:T(8,128)(2,1)}, u32[]{:S(2)}, u32[]{:S(2)}) async-start(bf16[16,256,1408]{1,0,2:T(8,128)(2,1)} %divide_convert_fusion.1), calls=%async_computation | async-start | bytes 23068672 | tf_op jit(solution)/shard_map/all_to_all | solution.py:25
  231.2 130.9 %all_gather.6 = bf16[2048,16]{0,1:T(8,128)(2,1)S(1)} all-gather(bf16[256,16]{0,1:T(8,128)(2,1)S(1)} %multiply_convert_fusion), channel_id=1, replica_groups=mesh['bank'=4,'zero'=8] {'zero'}, dimensions={0}, use_global_device_ids=true | all-gather | bytes 73728 | tf_op jit(solution)/shard_map/all_gather | solution.py:35
  362.1 14.0 %all_gather.7 = bf16[2048,64]{0,1:T(8,128)(2,1)S(1)} all-gather(bf16[2048,16]{0,1:T(8,128)(2,1)S(1)} %all_gather.6), channel_id=1, replica_groups=mesh['bank'=4,'zero'=8] {'bank'}, dimensions={1}, use_global_device_ids=true | all-gather | bytes 327680 | tf_op jit(solution)/shard_map/all_gather | solution.py:36
  376.1 0.7 constant_dynamic-slice_fusion
  376.7 0.7 constant_dynamic-slice_fusion.1
  377.4 11.4 %copy.24 = bf16[16,8,256,176]{2,1,3,0:T(8,128)(2,1)} copy(bf16[16,8,256,176]{2,0,3,1:T(8,128)(2,1)} %bitcast.5) | data formatting | bytes 23068672 | tf_op jit(solution)/shard_map/all_to_all | solution.py:26
  388.8 18.0 %all_to_all.33 = bf16[16,2048,176]{1,2,0:T(8,128)(2,1)} reshape(bf16[16,8,256,176]{2,1,3,0:T(8,128)(2,1)} %copy.24) | data formatting | bytes 23068672 | tf_op jit(solution)/shard_map/all_to_all | solution.py:26
  406.8 11.4 %copy.20 = bf16[16,8,256,176]{2,1,3,0:T(8,128)(2,1)} copy(bf16[16,8,256,176]{2,0,3,1:T(8,128)(2,1)} %bitcast.2) | data formatting | bytes 23068672 | tf_op jit(solution)/shard_map/all_to_all | solution.py:25
  418.1 18.0 %all_to_all.29 = bf16[16,2048,176]{1,2,0:T(8,128)(2,1)} reshape(bf16[16,8,256,176]{2,1,3,0:T(8,128)(2,1)} %copy.20) | data formatting | bytes 23068672 | tf_op jit(solution)/shard_map/all_to_all | solution.py:25
  436.1 0.7 copy.30
  (8 shorter events, 0.0 us)
Async XLA Ops:
  7.2 70.4 %all-reduce.3.cloned.1.call-start = ((), (), s32[]{:S(2)}) async-start(), calls=%async_computation.2 | async-start | bytes 180224 | tf_op jit(solution)/shard_map/psum | solution.py:11
  92.9 133.0 %all-to-all-start.1 = ((bf16[16,256,1408]{1,0,2:T(8,128)(2,1)}), bf16[16,256,1408]{1,0,2:T(8,128)(2,1)}, u32[]{:S(2)}, u32[]{:S(2)}) async-start(bf16[16,256,1408]{1,0,2:T(8,128)(2,1)} %divide_convert_fusion), calls=%async_computation.1 | async-start | bytes 23068672 | tf_op jit(solution)/shard_map/all_to_all | solution.py:26
  98.1 23.7 %copy-start = (bf16[16,1408]{1,0:T(8,128)(2,1)S(1)}, bf16[16,1408]{1,0:T(8,128)(2,1)}, u32[]{:S(2)}) copy-start(bf16[16,1408]{1,0:T(8,128)(2,1)} %get-tuple-element.5) | copy-start | bytes 135172
  122.1 109.1 %copy-start.1 = (f32[256,16]{0,1:T(8,128)S(1)}, f32[256,16]{0,1:T(8,128)}, u32[]{:S(2)}) copy-start(f32[256,16]{0,1:T(8,128)} %param.6) | copy-start | bytes 49156
  122.1 109.1 %copy-start.2 = (f32[256]{0:T(256)S(1)}, f32[256]{0:T(256)}, u32[]{:S(2)}) copy-start(f32[256]{0:T(256)} %param.7) | copy-start | bytes 3076
  225.9 180.9 %all-to-all-start = ((bf16[16,256,1408]{1,0,2:T(8,128)(2,1)}), bf16[16,256,1408]{1,0,2:T(8,128)(2,1)}, u32[]{:S(2)}, u32[]{:S(2)}) async-start(bf16[16,256,1408]{1,0,2:T(8,128)(2,1)} %divide_convert_fusion.1), calls=%async_computation | async-start | bytes 23068672 | tf_op jit(solution)/shard_map/all_to_all | solution.py:25
Sparse Core Ops, SparseCore 0:
  23.4 54.1 all-reduce.2
where the time goes:
time: 446 us; the launch traced here: 444 us
  blocking collectives  145 us (33%)
  waiting for transfers between devices  120 us (27%)
  local copies, waits for them, and re-layouts  109 us (24%)
  other arithmetic  45.3 us (10%)
  between operations  14.1 us (3%)
  starting transfers between devices  10.5 us (2%)
    all_gather x1, blocking collectives, local(): row_router = lax.all_gather(part_router, 'zero', axis=0, tiled=True)  131 us
    all_to_all x1, waiting for transfers between devices, local(): lax.all_to_all(narrow_up, 'zero', split_axis=2, concat_axis=1, tiled=True)  89.5 us
    unnamed x9, local copies, waits for them, and re-layouts  48.1 us
    psum x1, waiting for transfers between devices, local(): lax.psum(jnp.sum(jnp.abs(train_gate), axis=1).astype(jnp.bfloat16), 'zero')  30.6 us
    all_to_all x2, local copies, waits for them, and re-layouts, local(): lax.all_to_all(narrow_gate, 'zero', split_axis=2, concat_axis=1, tiled=True)  29.3 us
    all_to_all x2, local copies, waits for them, and re-layouts, local(): lax.all_to_all(narrow_up, 'zero', split_axis=2, concat_axis=1, tiled=True)  29.3 us
    reduce_sum x1, other arithmetic, local(): jnp.sum(jnp.abs(train_up), axis=1).astype(jnp.bfloat16)  16 us
    convert_element_type x1, other arithmetic, local(): (train_up / jnp.expand_dims(scale_up, 1)).astype(jnp.bfloat16)  14.2 us
  transfers between devices with their start and end apart: 3, of which 2 were waited for; matrix products, arithmetic and copies ran while one was open for 17% of the time, Pallas kernels for 0%

commit v1 on v0

--- a/solution.py
+++ b/solution.py
@@ -22,7 +22,12 @@
         (train_up / jnp.expand_dims(scale_up, 1)).astype(jnp.bfloat16),
     )
     ready_gate, ready_up = (
-        lax.all_to_all(narrow_gate, "zero", split_axis=2, concat_axis=1, tiled=True),
+        jnp.concatenate(
+            lax.all_to_all(
+                jnp.stack(jnp.split(narrow_gate, lax.axis_size("zero"), axis=2)), "zero", 0, 0
+            ),
+            axis=1,
+        ),
         lax.all_to_all(narrow_up, "zero", split_axis=2, concat_axis=1, tiled=True),
     )
     scale_gate = lax.dynamic_slice_in_dim(

time: 446 us -> 431 us (0.966)
  local copies, waits for them, and re-layouts: 109 us -> 98.2 us
  other arithmetic: 45.3 us -> 40.8 us
    all_to_all x1, waiting for transfers between devices: 0.01 us -> 89.6 us  [local(): lax.all_to_all(jnp.stack(jnp.split(narrow_gate, lax.axis_size('zero'), ax...]
    all_to_all x1, waiting for transfers between devices: 89.5 us -> 0.01 us  [local(): lax.all_to_all(narrow_up, 'zero', split_axis=2, concat_axis=1, tiled=True)]
    all_to_all x2 -> x0, local copies, waits for them, and re-layouts: 29.3 us -> none  [local(): lax.all_to_all(narrow_gate, 'zero', split_axis=2, concat_axis=1, tiled=True)]
    reshape x0 -> x1, local copies, waits for them, and re-layouts: none -> 10 us  [local(): jnp.concatenate(lax.all_to_all(jnp.stack(jnp.split(narrow_gate, lax.axis_...]
    unnamed x9 -> x16, local copies, waits for them, and re-layouts: 48.1 us -> 56.1 us
where the time goes in v1:
time: 431 us; the launch traced here: 429 us
  blocking collectives  145 us (34%)
  waiting for transfers between devices  121 us (28%)
  local copies, waits for them, and re-layouts  98.2 us (23%)
  other arithmetic  40.8 us (9%)
  between operations  14.1 us (3%)
  starting transfers between devices  10.5 us (2%)
    all_gather x1, blocking collectives, local(): row_router = lax.all_gather(part_router, 'zero', axis=0, tiled=True)  131 us
    all_to_all x1, waiting for transfers between devices, local(): lax.all_to_all(jnp.stack(jnp.split(narrow_gate, lax.axis_size('zero'), ax...  89.6 us
    unnamed x16, local copies, waits for them, and re-layouts  56.1 us
    psum x1, waiting for transfers between devices, local(): lax.psum(jnp.sum(jnp.abs(train_gate), axis=1).astype(jnp.bfloat16), 'zero')  31 us
    all_to_all x2, local copies, waits for them, and re-layouts, local(): lax.all_to_all(narrow_up, 'zero', split_axis=2, concat_axis=1, tiled=True)  29.3 us
    reduce_sum x1, other arithmetic, local(): jnp.sum(jnp.abs(train_up), axis=1).astype(jnp.bfloat16)  16 us
    convert_element_type x1, other arithmetic, local(): (train_up / jnp.expand_dims(scale_up, 1)).astype(jnp.bfloat16)  14.2 us
    all_gather x1, blocking collectives, local(): serve_router = lax.all_gather(row_router, 'bank', axis=1, tiled=True)  14 us
  transfers between devices with their start and end apart: 3, of which 2 were waited for; matrix products, arithmetic and copies ran while one was open for 17% of the time, Pallas kernels for 0%

profile of v1, /device:TPU:0, one launch (start us, length us, event | category | flops | bytes accessed | tf_op | source)
XLA Modules:
  0.0 429.2 jit_solution(7392823306983214482)
XLA Ops:
  7.2 16.0 %abs_reduce_fusion = (bf16[16,1408]{1,0:T(8,128)(2,1)}, bf16[16,1408]{1,0:T(8,128)(2,1)}) fusion(f32[16,256,1408]{2,1,0:T(8,128)} %param.5, f32[16,256,1408]{2,1,0:T(8,128)} %param.4), kind=kLoop, calls=%fused_computation.1 | loop fusion | flops 23023616 | bytes 46227456 | tf_op jit(solution)/shard_map/reduce_sum | solution.py:14
  23.3 23.3 %copy.21 = f32[16,256,1408]{1,2,0:T(8,128)} copy(f32[16,256,1408]{2,1,0:T(8,128)} %param.4) | data formatting | bytes 46137344 | tf_op args[0]
  46.6 31.0 %all-reduce.3.cloned.1.call-done = (bf16[16,1408]{1,0:T(8,128)(2,1)}, bf16[16,1408]{1,0:T(8,128)(2,1)}) async-done(((bf16[16,1408]{1,0:T(8,128)(2,1)}, bf16[16,1408]{1,0:T(8,128)(2,1)}), (bf16[16,1408]{1,0:T(8,128)(2,1)}, bf16[16,1408]{1,0:T(8,128)(2,1)})) %all-reduce.3.cloned.1.call-update) | async-done | bytes 90128 | tf_op jit(solution)/shard_map/psum | solution.py:11
  77.6 0.8 convert_multiply_fusion.1
  78.4 9.8 %divide_convert_fusion.1 = bf16[16,256,1408]{1,2,0:T(8,128)(2,1)S(1)} fusion(f32[16,256,1408]{1,2,0:T(8,128)} %copy.21, f32[16,1408]{1,0:T(8,128)S(1)} %convert_multiply_fusion.1), kind=kLoop, calls=%fused_computation.2 | loop fusion | flops 11534336 | bytes 34693120 | tf_op jit(solution)/shard_map/convert_element_type | solution.py:21
  88.2 1.2 fusion.7
  89.4 1.2 fusion.6
  90.6 1.2 fusion.5
  91.8 1.2 fusion.4
  93.0 1.2 fusion.3
  94.2 1.2 fusion.2
  95.4 1.2 fusion.1
  96.6 1.2 fusion
  97.8 5.2 %all-to-all-start = ((bf16[8,16,256,176]{2,3,1,0:T(8,128)(2,1)}), bf16[8,16,256,176]{2,3,1,0:T(8,128)(2,1)}, u32[]{:S(2)}, u32[]{:S(2)}) async-start(bf16[8,16,256,176]{2,3,1,0:T(8,128)(2,1)} %fusion), calls=%async_computation | async-start | bytes 23068672 | tf_op jit(solution)/shard_map/all_to_all | solution.py:26
  103.0 23.7 %copy.24 = f32[16,256,1408]{1,0,2:T(8,128)} copy(f32[16,256,1408]{2,1,0:T(8,128)} %param.5) | data formatting | bytes 46137344 | tf_op args[1]
  127.0 14.2 %divide_convert_fusion = bf16[16,256,1408]{1,0,2:T(8,128)(2,1)} fusion(f32[16,256,1408]{1,0,2:T(8,128)} %copy.24, f32[16,1408]{0,1:T(8,128)S(1)} %copy.23), kind=kLoop, calls=%fused_computation | loop fusion | flops 11534336 | bytes 34693120 | tf_op jit(solution)/shard_map/convert_element_type | solution.py:22
  141.2 89.6 %all-to-all-done = bf16[8,16,256,176]{2,3,1,0:T(8,128)(2,1)} async-done(((bf16[8,16,256,176]{2,3,1,0:T(8,128)(2,1)}), bf16[8,16,256,176]{2,3,1,0:T(8,128)(2,1)}, u32[]{:S(2)}, u32[]{:S(2)}) %all-to-all-start) | async-done | bytes 11534368 | tf_op jit(solution)/shard_map/all_to_all | solution.py:26
  230.8 5.3 %all-to-all-start.1 = ((bf16[16,256,1408]{1,0,2:T(8,128)(2,1)}), bf16[16,256,1408]{1,0,2:T(8,128)(2,1)}, u32[]{:S(2)}, u32[]{:S(2)}) async-start(bf16[16,256,1408]{1,0,2:T(8,128)(2,1)} %divide_convert_fusion), calls=%async_computation.1 | async-start | bytes 23068672 | tf_op jit(solution)/shard_map/all_to_all | solution.py:31
  236.1 130.9 %all_gather.6 = bf16[2048,16]{0,1:T(8,128)(2,1)S(1)} all-gather(bf16[256,16]{0,1:T(8,128)(2,1)S(1)} %multiply_convert_fusion), channel_id=1, replica_groups=mesh['bank'=4,'zero'=8] {'zero'}, dimensions={0}, use_global_device_ids=true | all-gather | bytes 73728 | tf_op jit(solution)/shard_map/all_gather | solution.py:40
  367.0 14.0 %all_gather.7 = bf16[2048,64]{0,1:T(8,128)(2,1)S(1)} all-gather(bf16[2048,16]{0,1:T(8,128)(2,1)S(1)} %all_gather.6), channel_id=1, replica_groups=mesh['bank'=4,'zero'=8] {'bank'}, dimensions={1}, use_global_device_ids=true | all-gather | bytes 327680 | tf_op jit(solution)/shard_map/all_gather | solution.py:41
  382.3 10.0 %copy.28 = bf16[8,16,22,8,256]{4,3,0,2,1:T(8,128)(2,1)} copy(bf16[8,16,22,8,256]{4,3,2,1,0:T(8,128)(2,1)} %bitcast.12) | data formatting | bytes 23068672 | tf_op jit(solution)/shard_map/reshape | solution.py:25
  392.3 11.4 %copy.26 = bf16[16,8,256,176]{2,1,3,0:T(8,128)(2,1)} copy(bf16[16,8,256,176]{2,0,3,1:T(8,128)(2,1)} %bitcast.11) | data formatting | bytes 23068672 | tf_op jit(solution)/shard_map/all_to_all | solution.py:31
  403.7 18.0 %all_to_all.20 = bf16[16,2048,176]{1,2,0:T(8,128)(2,1)} reshape(bf16[16,8,256,176]{2,1,3,0:T(8,128)(2,1)} %copy.26) | data formatting | bytes 23068672 | tf_op jit(solution)/shard_map/all_to_all | solution.py:31
  421.6 0.7 copy.39
  (14 shorter events, 1.7 us)
Async XLA Ops:
  7.2 70.4 %all-reduce.3.cloned.1.call-start = ((), (), s32[]{:S(2)}) async-start(), calls=%async_computation.2 | async-start | bytes 180224 | tf_op jit(solution)/shard_map/psum | solution.py:11
  97.8 133.0 %all-to-all-start = ((bf16[8,16,256,176]{2,3,1,0:T(8,128)(2,1)}), bf16[8,16,256,176]{2,3,1,0:T(8,128)(2,1)}, u32[]{:S(2)}, u32[]{:S(2)}) async-start(bf16[8,16,256,176]{2,3,1,0:T(8,128)(2,1)} %fusion), calls=%async_computation | async-start | bytes 23068672 | tf_op jit(solution)/shard_map/all_to_all | solution.py:26
  103.0 23.7 %copy-start = (bf16[16,1408]{1,0:T(8,128)(2,1)S(1)}, bf16[16,1408]{1,0:T(8,128)(2,1)}, u32[]{:S(2)}) copy-start(bf16[16,1408]{1,0:T(8,128)(2,1)} %get-tuple-element.6) | copy-start | bytes 135172
  141.2 94.9 %copy-start.1 = (f32[256,16]{0,1:T(8,128)S(1)}, f32[256,16]{0,1:T(8,128)}, u32[]{:S(2)}) copy-start(f32[256,16]{0,1:T(8,128)} %param.6) | copy-start | bytes 49156
  141.2 94.9 %copy-start.2 = (f32[256]{0:T(256)S(1)}, f32[256]{0:T(256)}, u32[]{:S(2)}) copy-start(f32[256]{0:T(256)} %param.7) | copy-start | bytes 3076
  230.8 161.6 %all-to-all-start.1 = ((bf16[16,256,1408]{1,0,2:T(8,128)(2,1)}), bf16[16,256,1408]{1,0,2:T(8,128)(2,1)}, u32[]{:S(2)}, u32[]{:S(2)}) async-start(bf16[16,256,1408]{1,0,2:T(8,128)(2,1)} %divide_convert_fusion), calls=%async_computation.1 | async-start | bytes 23068672 | tf_op jit(solution)/shard_map/all_to_all | solution.py:31
Sparse Core Ops, SparseCore 0:
  23.4 54.1 all-reduce.2
